TPU v7x, 256 devices: a whole 4x4x8 slice. The times are simulated.
256 devices in a mesh: first: 16 (over y, x), second: 16 (over z, core).
Axes of the slice: x: 4, y: 4, z: 8, core: 2. Of those that a mesh axis runs over, the one named last changes fastest.
Arguments:
- pair_state: bfloat16 [768, 768, 128], P('first', 'second'), may hold values from -6 to 6
- in_gain: float32 [128], replicated, may hold values from 0.25 to 1.75
- left_weight: bfloat16 [128, 128], replicated, may hold values from -0.5 to 0.5
- right_weight: bfloat16 [128, 128], replicated, may hold values from -0.5 to 0.5
- mid_gain: float32 [128], replicated, may hold values from 0.25 to 1.75
- out_weight: bfloat16 [128, 128], replicated, may hold values from -0.5 to 0.5
- out_gate: bfloat16 [128, 128], replicated, may hold values from -0.5 to 0.5
Outputs:
- triangle_out: bfloat16 [768, 768, 128], P('first', 'second')
All inputs are finite; a program needn't handle non-finite values.
Results may differ from a plain program's by a relative error of at most 0.015.
Values may be sent and summed in bfloat16 or wider, within the bound.
A program may use at most 64 MiB of HBM per device.

v0:
```python
import jax
import jax.numpy as jnp
from jax import lax
from jax.sharding import PartitionSpec as P


def unit_channels(values, channel_gain):
    centred = values - jnp.mean(values, axis=-1, keepdims=True)
    return (
        centred
        * lax.rsqrt(jnp.mean(centred * centred, axis=-1, keepdims=True) + 1e-05)
        * channel_gain
    )


def make_factors(pair_in, in_gain, left_weight, right_weight):
    ready = unit_channels(pair_in.astype(jnp.float32), in_gain).astype(jnp.bfloat16)
    ready = lax.optimization_barrier(ready)
    left = jnp.einsum("ijc,cd->ijd", ready, left_weight, preferred_element_type=jnp.float32)
    right = jnp.einsum("ijc,cd->ijd", ready, right_weight, preferred_element_type=jnp.float32)
    return (ready, left.astype(jnp.bfloat16), right.astype(jnp.bfloat16))


def finish_pair(mixed, ready, mid_gain, out_weight, out_gate):
    scaled = unit_channels(mixed.astype(jnp.float32), mid_gain).astype(jnp.bfloat16)
    scaled = lax.optimization_barrier(scaled)
    gate = jax.nn.sigmoid(
        jnp.einsum("ijc,cd->ijd", ready, out_gate, preferred_element_type=jnp.float32)
    )
    return (
        jnp.einsum("ijd,dc->ijc", scaled, out_weight, preferred_element_type=jnp.float32) * gate
    ).astype(jnp.bfloat16)


def per_device(pair_state, in_gain, left_weight, right_weight, mid_gain, out_weight, out_gate):
    ready, left, right = make_factors(pair_state, in_gain, left_weight, right_weight)
    count = pair_state.shape[1] * lax.axis_size("second")
    left_lines, right_lines = (
        lax.all_to_all(left, "second", split_axis=2, concat_axis=1, tiled=True),
        lax.all_to_all(right, "second", split_axis=2, concat_axis=1, tiled=True),
    )

    def meet(piece):
        return jnp.einsum("ikd,jkd->ijd", left_lines, piece, preferred_element_type=jnp.float32)

    strip = meet(lax.all_gather(right_lines, "first", axis=0, tiled=True))
    strip = (strip * count ** (-0.5)).astype(jnp.bfloat16)
    mixed = lax.all_to_all(strip, "second", split_axis=1, concat_axis=2, tiled=True)
    return finish_pair(mixed, ready, mid_gain, out_weight, out_gate)


def solution(mesh):
    in_specs = (P("first", "second", None), P(), P(), P(), P(), P(), P())
    out_specs = P("first", "second", None)
    return jax.shard_map(
        per_device, mesh=mesh, in_specs=in_specs, out_specs=out_specs, check_vma=False
    )
```

profile of v0, /device:TPU:1, one launch (start us, length us, event | category | flops | bytes accessed | tf_op | source)
XLA Modules:
  0.0 180.6 jit_solution(738637115696771919)
XLA Ops:
  6.5 0.0 copy-start
  6.5 0.0 all-gather.2.cloned.1.call-start
  6.5 1.5 convert_reduce_fusion
  8.1 1.8 fusion.13
  9.9 0.0 copy-done.1
  9.9 1.4 fusion.15
  11.3 0.0 copy-start.2
  11.3 0.8 copy-done.2
  12.1 0.0 copy-done
  12.1 0.3 convolution_convert_fusion.1
  12.4 1.0 copy.17
  13.4 2.4 %reshape.39 = bf16[16,2,9216]{2,1,0:T(2,128)(2,1)S(1)} reshape(bf16[128,48,48]{2,1,0:T(8,128)(2,1)S(1)} %bitcast.60) | data formatting | bytes 1179648
  15.8 28.4 %all_to_all.45 = bf16[16,2,9216]{2,1,0:T(2,128)(2,1)S(1)} all-to-all(bf16[16,2,9216]{2,1,0:T(2,128)(2,1)S(1)} %reshape.39), channel_id=1, replica_groups=mesh['first'=16,'second'=16] {'second'}, dimensions={0} | all-to-all | bytes 1179648 | tf_op jit(solution)/shard_map/all_to_all | solution.py:40
  44.2 1.5 reshape.40
  45.8 1.0 copy.19
  46.8 0.0 copy-start.3
  46.8 0.0 copy-start.7
  46.8 2.3 %all_to_all.36 = bf16[48,768,8]{1,0,2:T(8,128)(2,1)} reshape(bf16[48,16,48,8]{2,1,0,3:T(8,128)(2,1)S(1)} %copy.19) | data formatting | bytes 1179648 | tf_op jit(solution)/shard_map/all_to_all | solution.py:40
  49.1 0.0 all-gather.2.cloned.1.call-update
  49.1 0.0 copy-done.3
  49.1 0.0 copy-done.7
  49.1 0.3 convolution_convert_fusion
  49.4 1.0 copy.20
  50.4 2.4 %reshape.41 = bf16[16,2,9216]{2,1,0:T(2,128)(2,1)S(1)} reshape(bf16[128,48,48]{2,1,0:T(8,128)(2,1)S(1)} %bitcast.61) | data formatting | bytes 1179648
  52.8 21.8 %all_to_all.46 = bf16[16,2,9216]{2,1,0:T(2,128)(2,1)S(1)} all-to-all(bf16[16,2,9216]{2,1,0:T(2,128)(2,1)S(1)} %reshape.41), channel_id=1, replica_groups=mesh['first'=16,'second'=16] {'second'}, dimensions={0} | all-to-all | bytes 1179648 | tf_op jit(solution)/shard_map/all_to_all | solution.py:39
  74.5 1.5 reshape.42
  76.1 1.0 copy.22
  77.1 1.6 all_to_all.40
  78.7 47.9 %all-gather.2.cloned.1.call-done = bf16[768,768,8]{1,0,2:T(8,128)(2,1)} async-done(((bf16[48,768,8]{1,0,2:T(8,128)(2,1)}), bf16[768,768,8]{1,0,2:T(8,128)(2,1)}) %all-gather.2.cloned.1.call-update) | async-done | bytes 9437200 | tf_op jit(solution)/shard_map/all_gather | solution.py:46
  126.5 6.5 %fusion.12 = bf16[48,768,8]{1,0,2:T(8,128)(2,1)S(1)} fusion(bf16[768,768,8]{1,0,2:T(8,128)(2,1)} %all-gather.2.cloned.1.call-done, bf16[48,768,8]{1,0,2:T(8,128)(2,1)S(1)} %all_to_all.40), kind=kOutput, calls=%fused_computation.22 | convolution fusion | flops 453574656 | bytes 10616832 | tf_op jit(solution)/shard_map/ikd,jkd->ijd/dot_general | solution.py:44
  133.1 1.1 copy.23
  134.2 0.0 copy-start.4
  134.2 0.0 copy-start.9
  134.2 3.1 %reshape.43 = bf16[16,2,9216]{2,1,0:T(2,128)(2,1)} reshape(bf16[768,8,48]{2,1,0:T(8,128)(2,1)S(1)} %bitcast.62) | data formatting | bytes 1179648
  137.3 7.9 %all-to-all-start.2 = ((bf16[16,2,9216]{2,1,0:T(2,128)(2,1)}), bf16[16,2,9216]{2,1,0:T(2,128)(2,1)S(1)}, u32[]{:S(2)}, u32[]{:S(2)}) async-start(bf16[16,2,9216]{2,1,0:T(2,128)(2,1)} %reshape.43), calls=%async_computation.2 | async-start | bytes 1179648 | tf_op jit(solution)/shard_map/all_to_all | solution.py:48
  145.2 0.0 copy-done.4
  145.2 0.0 copy-done.9
  145.2 1.5 fusion.9
  146.7 16.8 %all-to-all-done.2 = bf16[16,2,9216]{2,1,0:T(2,128)(2,1)S(1)} async-done(((bf16[16,2,9216]{2,1,0:T(2,128)(2,1)}), bf16[16,2,9216]{2,1,0:T(2,128)(2,1)S(1)}, u32[]{:S(2)}, u32[]{:S(2)}) %all-to-all-start.2) | async-done | bytes 589856 | tf_op jit(solution)/shard_map/all_to_all | solution.py:48
  163.5 2.4 %reshape.44 = bf16[768,8,48]{2,1,0:T(8,128)(2,1)} reshape(bf16[16,2,9216]{2,1,0:T(2,128)(2,1)S(1)} %all-to-all-done.2) | data formatting | bytes 1179648
  166.0 4.1 %copy.24 = f32[48,16,48,8]{2,3,1,0:T(8,128)S(1)} copy(bf16[48,16,48,8]{0,3,2,1:T(8,128)(2,1)} %bitcast.63) | data formatting | bytes 1769472 | tf_op jit(solution)/shard_map/convert_element_type | solution.py:25
  170.0 0.4 bitcast_reduce_fusion
  170.4 0.0 copy-start.8
  170.4 0.6 fusion.4
  171.0 0.0 copy-done.8
  171.1 0.7 fusion.2
  171.8 0.5 copy-done.5
  172.4 1.4 fusion.10
  (8 shorter events, 0.0 us)
Async XLA Ops:
  6.5 5.6 %copy-start = (bf16[128,128]{1,0:T(8,128)(2,1)S(1)}, bf16[128,128]{1,0:T(8,128)(2,1)}, u32[]{:S(2)}) copy-start(bf16[128,128]{1,0:T(8,128)(2,1)} %param.10) | copy-start | bytes 98308
  6.5 3.3 %copy-start.1 = (bf16[48,48,128]{2,1,0:T(8,128)(2,1)S(1)}, bf16[48,48,128]{2,1,0:T(8,128)(2,1)}, u32[]{:S(2)}) copy-start(bf16[48,48,128]{2,1,0:T(8,128)(2,1)} %param.7) | copy-start | bytes 1769476
  6.5 120.0 %all-gather.2.cloned.1.call-start = ((), (), s32[]{:S(2)}) async-start(), calls=%async_computation.3 | async-start | bytes 10027008 | tf_op jit(solution)/shard_map/all_gather | solution.py:46
  11.3 0.8 copy-start.2
  46.8 2.3 %copy-start.3 = (bf16[48,48,128]{2,1,0:T(8,128)(2,1)S(1)}, bf16[48,48,128]{2,1,0:T(8,128)(2,1)}, u32[]{:S(2)}) copy-start(bf16[48,48,128]{2,1,0:T(8,128)(2,1)} %copy-done.2) | copy-start | bytes 1769476
  46.8 2.3 %copy-start.7 = (bf16[128,128]{1,0:T(8,128)(2,1)S(1)}, bf16[128,128]{1,0:T(8,128)(2,1)}, u32[]{:S(2)}) copy-start(bf16[128,128]{1,0:T(8,128)(2,1)} %param.9) | copy-start | bytes 98308
  134.2 11.1 %copy-start.4 = (bf16[48,48,128]{2,1,0:T(8,128)(2,1)S(1)}, bf16[48,48,128]{2,1,0:T(8,128)(2,1)}, u32[]{:S(2)}) copy-start(bf16[48,48,128]{2,1,0:T(8,128)(2,1)} %copy-done.2) | copy-start | bytes 1769476
  134.2 11.0 %copy-start.9 = (bf16[128,128]{1,0:T(8,128)(2,1)S(1)}, bf16[128,128]{1,0:T(8,128)(2,1)}, u32[]{:S(2)}) copy-start(bf16[128,128]{1,0:T(8,128)(2,1)} %param.13) | copy-start | bytes 98308
  137.3 26.3 %all-to-all-start.2 = ((bf16[16,2,9216]{2,1,0:T(2,128)(2,1)}), bf16[16,2,9216]{2,1,0:T(2,128)(2,1)S(1)}, u32[]{:S(2)}, u32[]{:S(2)}) async-start(bf16[16,2,9216]{2,1,0:T(2,128)(2,1)} %reshape.43), calls=%async_computation.2 | async-start | bytes 1179648 | tf_op jit(solution)/shard_map/all_to_all | solution.py:48
  170.4 0.7 copy-start.8
  171.1 1.3 copy-start.5
  171.1 1.3 copy-start.6
Sparse Core Ops, SparseCore 0:
  49.2 77.2 all-gather.1
where the time goes:
time: 181 us
  waiting for transfers between devices  64.7 us (36%)
  blocking collectives  50.2 us (28%)
  local copies, waits for them, and re-layouts  27.7 us (15%)
  between operations  13.7 us (8%)
  matrix products  9.99 us (6%)
  starting transfers between devices  7.95 us (4%)
  other arithmetic  6.45 us (4%)
    all_gather x1, waiting for transfers between devices, per_device(): strip = meet(lax.all_gather(right_lines, 'first', axis=0, tiled=True))  47.9 us
    all_to_all x1, blocking collectives, per_device(): lax.all_to_all(right, 'second', split_axis=2, concat_axis=1, tiled=True)  28.4 us
    all_to_all x1, blocking collectives, per_device(): lax.all_to_all(left, 'second', split_axis=2, concat_axis=1, tiled=True)  21.8 us
    all_to_all x1, waiting for transfers between devices, per_device(): lax.all_to_all(strip, 'second', split_axis=1, concat_axis=2, tiled=True)  16.8 us
    unnamed x26, local copies, waits for them, and re-layouts  14.7 us
    all_to_all x1, starting transfers between devices, per_device(): lax.all_to_all(strip, 'second', split_axis=1, concat_axis=2, tiled=True)  7.95 us
    dot_general x1, matrix products, meet(): jnp.einsum('ikd,jkd->ijd', left_lines, piece, preferred_element_type=jnp....  6.53 us
    convert_element_type x1, local copies, waits for them, and re-layouts, finish_pair(): mixed.astype(jnp.float32)  4.06 us
  transfers between devices with their start and end apart: 2, of which 2 were waited for; matrix products, arithmetic and copies ran while one was open for 4% of the time, Pallas kernels for 0%

commit v1 on v0

v1 whole, which is shorter than its diff:
```python
import functools

import jax
import jax.numpy as jnp
from jax import lax
from jax.experimental import pallas as pl
from jax.experimental.pallas import tpu as pltpu
from jax.sharding import PartitionSpec as P

MESH = pl.DeviceIdType.MESH
NX, NY, NS = 4, 4, 16
BLK = 48
SUB = 16
NP = BLK // SUB
W = 128
KALL = BLK * NS
HALF_L = KALL // 2
HALF_R = W // 2


def unit_channels(values, channel_gain):
    centred = values - jnp.mean(values, axis=-1, keepdims=True)
    return (
        centred
        * lax.rsqrt(jnp.mean(centred * centred, axis=-1, keepdims=True) + 1e-05)
        * channel_gain
    )


def butterfly(slabs, first_stride):
    n = len(slabs)
    lane = lax.broadcasted_iota(jnp.int32, slabs[0].shape, 1)
    bit = 1
    while bit < n:
        stride = bit * first_stride
        low = (lane // stride) % 2 == 0
        out = list(slabs)
        for a in range(n):
            if a & bit:
                continue
            b = a | bit
            u, v = slabs[a], slabs[b]
            out[a] = jnp.where(low, u, pltpu.roll(v, stride, 1))
            out[b] = jnp.where(low, pltpu.roll(u, W - stride, 1), v)
        slabs = out
        bit *= 2
    return slabs


def kernel(
    x_ref, in_gain, left_w, right_w, mid_gain, out_w, out_gate,
    o_ref,
    ready, gate, send_l, send_r, land_r, left_g, right_g, stage, land_o,
    zs, zr, gs, gr, os_, or_,
):
    f, s = lax.axis_index("first"), lax.axis_index("second")
    y, x = f // NX, f % NX

    def dev(first, second):
        return {"first": first, "second": second}

    xp, xm = y * NX + (x + 1) % NX, y * NX + (x + NX - 1) % NX
    yp, ym = ((y + 1) % NY) * NX + x, ((y + NY - 1) % NY) * NX + x
    column = s % NX
    own = column == x

    barrier = pltpu.get_barrier_semaphore()

    def greet(first, second):
        pl.semaphore_signal(barrier, inc=1, device_id=dev(first, second), device_id_type=MESH)

    def greet_line(t, carry):
        greet(f, (s + t) % NS)
        return carry

    lax.fori_loop(1, NS, greet_line, 0)
    for peer in (xp, xm, yp, ym):
        greet(peer, s)

    def greet_senders(t, carry):
        first = y * NX + column

        @pl.when(jnp.logical_or(first != f, t != s))
        def _():
            greet(first, t)

        return carry

    lax.fori_loop(0, NS, greet_senders, 0)

    rows = lax.broadcasted_iota(jnp.int32, (W, W), 0)
    cols = lax.broadcasted_iota(jnp.int32, (W, W), 1)
    swap = (rows == (cols % 16) * 8 + cols // 16).astype(jnp.bfloat16)
    right_mix = jnp.dot(
        right_w[...], swap, preferred_element_type=jnp.float32
    ).astype(jnp.bfloat16)

    def line_copy(t, p, which):
        h = (t // 2 + 1) // 2 * (2 * ((t // 2) % 2) - 1)
        to = ((s // 2 + h + 8) % 8) * 2 + (s + t) % 2
        if which == 0:
            src, dst = send_l.at[to, p], left_g.at[p, x, pl.ds(pl.multiple_of(s * BLK, BLK), BLK)]
        else:
            src, dst = send_r.at[to, p], land_r.at[p, pl.ds(pl.multiple_of(s * BLK, BLK), BLK)]
        return pltpu.make_async_remote_copy(
            src_ref=src, dst_ref=dst, send_sem=zs.at[p, which], recv_sem=zr.at[p, which],
            device_id=dev(f, to), device_id_type=MESH,
        )

    def line_local(p, which):
        if which == 0:
            src, dst = send_l.at[s, p], left_g.at[p, x, pl.ds(pl.multiple_of(s * BLK, BLK), BLK)]
        else:
            src, dst = send_r.at[s, p], land_r.at[p, pl.ds(pl.multiple_of(s * BLK, BLK), BLK)]
        return pltpu.make_async_copy(src, dst, zr.at[p, which])

    def factor_piece(p):
        at = pl.multiple_of(p * SUB, SUB)
        values = x_ref[pl.ds(at, SUB)].reshape(SUB * BLK, W).astype(jnp.float32)
        r = unit_channels(values, in_gain[...]).astype(jnp.bfloat16)
        ready[pl.ds(at, SUB)] = r.reshape(SUB, BLK, W)
        for which, weight, stride, buf in ((0, left_w[...], 8, send_l), (1, right_mix, 1, send_r)):
            full = jnp.dot(r, weight, preferred_element_type=jnp.float32)
            full = full.astype(jnp.bfloat16).reshape(SUB, BLK, W)
            slabs = butterfly([full[i] for i in range(SUB)], stride)
            for i in range(SUB):
                buf[i, p] = slabs[i]

    def send_piece(p):
        for which in (0, 1):
            line_local(p, which).start()

            def go(t, carry, which=which):
                line_copy(t, p, which).start()
                return carry

            lax.fori_loop(1, NS, go, 0)

    factor_piece(0)
    pl.semaphore_wait(barrier, (NS - 1) + 4 + NS - own.astype(jnp.int32))

    def piece(p, carry):
        @pl.when(p > 0)
        def _():
            factor_piece(p)

        send_piece(p)
        return carry

    lax.fori_loop(0, NP, piece, 0)

    def gate_rows(i, carry):
        at = pl.multiple_of(i * SUB, SUB)
        r = ready[pl.ds(at, SUB)].reshape(SUB * BLK, W)
        g = jax.nn.sigmoid(jnp.dot(r, out_gate[...], preferred_element_type=jnp.float32))
        gate[pl.ds(at, SUB)] = g.reshape(SUB, BLK, W)
        return carry

    lax.fori_loop(0, NP, gate_rows, 0)

    def gather_copy(p, which, k):
        n = NX if which == 0 else NY
        at = x if which == 0 else y
        buf = left_g if which == 0 else right_g
        half = HALF_L if which == 0 else HALF_R
        up, down = (xp, xm) if which == 0 else (yp, ym)
        if k == 0 or k == 1:
            ref = buf.at[p, at]
        elif k == 2:
            ref = buf.at[p, (at + n - 1) % n, pl.ds(0, half)]
        else:
            ref = buf.at[p, (at + 1) % n, pl.ds(half, half)]
        return pltpu.make_async_remote_copy(
            src_ref=ref, dst_ref=ref, send_sem=gs.at[p, which, k], recv_sem=gr.at[p, which, k],
            device_id=dev(up if k % 2 == 0 else down, s), device_id_type=MESH,
        )

    def line_arrived(p, which):
        ref = left_g.at[p, x] if which == 0 else land_r.at[p]
        pltpu.make_async_copy(ref, ref, zr.at[p, which]).wait()

    def gather_first(p):
        line_arrived(p, 0)
        for k in (0, 1):
            gather_copy(p, 0, k).start()
        line_arrived(p, 1)
        right_g[p, y] = jnp.transpose(land_r[p])
        for k in (0, 1):
            gather_copy(p, 1, k).start()

    def gather_second(p):
        for which in (0, 1):
            for k in (0, 1):
                gather_copy(p, which, k).wait_recv()
                gather_copy(p, which, k + 2).start()

    def gather_last(p):
        for which in (0, 1):
            for k in (2, 3):
                gather_copy(p, which, k).wait_recv()

    lane_channel = lax.broadcasted_iota(jnp.int32, (SUB, W), 1) % 8

    def product(a, b):
        def one(v, carry):
            right = right_g[b, v]
            for h in range(2):
                left = jnp.concatenate([left_g[a, 2 * h], left_g[a, 2 * h + 1]], axis=1)
                full = jnp.dot(right, left, preferred_element_type=jnp.float32)
                for u in range(2):
                    tile = full[:, u * W : (u + 1) * W]
                    res = tile[:SUB]
                    for d in range(1, 8):
                        res = jnp.where(lane_channel == d, tile[d * SUB : (d + 1) * SUB], res)
                    res = (res * KALL ** (-0.5)).astype(jnp.bfloat16)
                    stage[(2 * h + u) * NY + v, a, pl.ds(pl.multiple_of(b * SUB, SUB), SUB)] = res
            return carry

        lax.fori_loop(0, NY, one, 0)

    runs = ((0, 0, 1), (0, 1, 1), (1, 0, 2), (0, 2, 1), (1, 2, 1), (2, 0, 3))

    def send_run(n):
        a, b, count = runs[n]
        sl = pl.ds(b * SUB, count * SUB)

        def go(t, carry):
            u, v = t // NY, t % NY
            u, v = (x + u) % NX, (s // NX + v) % NY
            first, second = y * NX + u, v * NX + x
            src, dst = stage.at[u * NY + v, a, sl], land_o.at[s, a, sl]
            mine = jnp.logical_and(first == f, second == s)

            @pl.when(mine)
            def _():
                pltpu.make_async_copy(src, dst, or_.at[n]).start()

            @pl.when(jnp.logical_not(mine))
            def _():
                pltpu.make_async_remote_copy(
                    src_ref=src, dst_ref=dst, send_sem=os_.at[n], recv_sem=or_.at[n],
                    device_id=dev(first, second), device_id_type=MESH,
                ).start()

            return carry

        lax.fori_loop(0, NX * NY, go, 0)

    def run_arrived(n):
        a, b, count = runs[n]
        ref = land_o.at[:, a, pl.ds(b * SUB, count * SUB)]
        pltpu.make_async_copy(ref, ref, or_.at[n]).wait()

    def finish(a, b):
        at = pl.ds(pl.multiple_of(b * SUB, SUB), SUB)
        slabs = butterfly([land_o[i, a, at] for i in range(NS)], 8)
        mixed = jnp.concatenate(slabs, axis=0).astype(jnp.float32)
        scaled = unit_channels(mixed, mid_gain[...]).astype(jnp.bfloat16)
        res = jnp.dot(scaled, out_w[...], preferred_element_type=jnp.float32)
        rows_ = pl.ds(pl.multiple_of(a * SUB, SUB), SUB)
        o_ref[rows_, at] = (res.reshape(SUB, SUB, W) * gate[rows_, at]).astype(jnp.bfloat16)

    gather_first(0)
    gather_second(0)
    gather_first(1)
    gather_last(0)
    product(0, 0)
    send_run(0)
    gather_second(1)
    gather_first(2)
    gather_last(1)
    product(0, 1)
    send_run(1)

    def more(b, carry):
        product(1, b)
        return carry

    lax.fori_loop(0, 2, more, 0)
    send_run(2)
    gather_second(2)
    gather_last(2)
    product(0, 2)
    send_run(3)
    product(1, 2)
    send_run(4)

    def most(b, carry):
        product(2, b)
        return carry

    lax.fori_loop(0, 3, most, 0)
    send_run(5)

    for n in range(6):
        run_arrived(n)
        a, b, count = runs[n]

        def fin(i, carry, a=a, b=b):
            finish(a, b + i)
            return carry

        lax.fori_loop(0, count, fin, 0)

    for p in range(NP):
        for which in (0, 1):
            buf = (send_l, send_r)[which]
            ref = buf.at[pl.ds(0, NS - 1), p]
            pltpu.make_async_copy(ref, ref, zs.at[p, which]).wait()
            for k in range(4):
                gather_copy(p, which, k).wait_send()
    for n in range(6):
        a, b, count = runs[n]
        sl = pl.ds(b * SUB, count * SUB)

        @pl.when(own)
        def _(n=n, a=a, sl=sl):
            ref = stage.at[pl.ds(0, NX * NY - 1), a, sl]
            pltpu.make_async_copy(ref, ref, os_.at[n]).wait()

        @pl.when(jnp.logical_not(own))
        def _(n=n, a=a, sl=sl):
            ref = stage.at[:, a, sl]
            pltpu.make_async_copy(ref, ref, os_.at[n]).wait()


def per_device(pair_state, in_gain, left_weight, right_weight, mid_gain, out_weight, out_gate):
    bf = jnp.bfloat16
    vmem = pl.BlockSpec(memory_space=pltpu.VMEM)
    return pl.pallas_call(
        kernel,
        out_shape=jax.ShapeDtypeStruct((BLK, BLK, W), bf),
        in_specs=[vmem] * 7,
        out_specs=vmem,
        scratch_shapes=[
            pltpu.VMEM((BLK, BLK, W), bf),
            pltpu.VMEM((BLK, BLK, W), jnp.float32),
            pltpu.VMEM((NS, NP, BLK, W), bf),
            pltpu.VMEM((NS, NP, BLK, W), bf),
            pltpu.VMEM((NP, KALL, W), bf),
            pltpu.VMEM((NP, NX, KALL, W), bf),
            pltpu.VMEM((NP, NY, W, KALL), bf),
            pltpu.VMEM((NX * NY, NP, BLK, W), bf),
            pltpu.VMEM((NS, NP, BLK, W), bf),
            pltpu.SemaphoreType.DMA((NP, 2)),
            pltpu.SemaphoreType.DMA((NP, 2)),
            pltpu.SemaphoreType.DMA((NP, 2, 4)),
            pltpu.SemaphoreType.DMA((NP, 2, 4)),
            pltpu.SemaphoreType.DMA((6,)),
            pltpu.SemaphoreType.DMA((6,)),
        ],
        compiler_params=pltpu.CompilerParams(
            collective_id=0, has_side_effects=True, vmem_limit_bytes=48 * 1024 * 1024
        ),
    )(pair_state, in_gain.reshape(1, W), left_weight, right_weight, mid_gain.reshape(1, W), out_weight, out_gate)


def solution(mesh):
    in_specs = (P("first", "second", None), P(), P(), P(), P(), P(), P())
    out_specs = P("first", "second", None)
    return jax.shard_map(
        per_device, mesh=mesh, in_specs=in_specs, out_specs=out_specs, check_vma=False
    )
```

time: 181 us -> 75.8 us (0.42)
  Pallas kernels: 0 us -> 69.8 us
  waiting for transfers between devices: 64.7 us -> 0 us
  blocking collectives: 50.2 us -> 0 us
  local copies, waits for them, and re-layouts: 27.7 us -> 5.58 us
  between operations: 13.7 us -> 0.02 us
  matrix products: 9.99 us -> 0 us
  starting transfers between devices: 7.95 us -> 0 us
  other arithmetic: 6.45 us -> 0 us
    pallas_call x0 -> x1, Pallas kernels: none -> 69.8 us  [per_device(): pl.pallas_call(kernel, out_shape=jax.ShapeDtypeStruct((BLK, BLK, W), bf),...]
    all_to_all x2 -> x0, blocking collectives: 50.2 us -> none  [the longest x1 28.4 us: per_device(): lax.all_to_all(right, 'second', split_axis=2, concat_axis=1, tiled=True)]
    all_gather x1 -> x0, waiting for transfers between devices: 47.9 us -> none  [per_device(): strip = meet(lax.all_gather(right_lines, 'first', axis=0, tiled=True))]
    all_to_all x1 -> x0, waiting for transfers between devices: 16.8 us -> none  [per_device(): lax.all_to_all(strip, 'second', split_axis=1, concat_axis=2, tiled=True)]
    dot_general x5 -> x0, matrix products: 9.99 us -> none  [the longest x1 6.53 us: meet(): jnp.einsum('ikd,jkd->ijd', left_lines, piece, preferred_element_type=jnp....]
    unnamed x26 -> x15, local copies, waits for them, and re-layouts: 14.7 us -> 5.58 us
    all_to_all x1 -> x0, starting transfers between devices: 7.95 us -> none  [per_device(): lax.all_to_all(strip, 'second', split_axis=1, concat_axis=2, tiled=True)]
    convert_element_type x4 -> x0, local copies, waits for them, and re-layouts: 7.08 us -> none  [the longest x1 4.06 us: finish_pair(): mixed.astype(jnp.float32)]
  transfers between devices with their start and end apart: 2 -> 0, of which waited for: 2 -> 0; matrix products, arithmetic and copies ran while one was open for 4% -> 0% of each run, Pallas kernels for 0% -> 0%
where the time goes in v1:
time: 75.8 us; the launch traced here: 75.4 us
  Pallas kernels  69.8 us (92%)
  local copies, waits for them, and re-layouts  5.58 us (7%)
    pallas_call x1, Pallas kernels, per_device(): pl.pallas_call(kernel, out_shape=jax.ShapeDtypeStruct((BLK, BLK, W), bf),...  69.8 us
    unnamed x15, local copies, waits for them, and re-layouts  5.58 us

profile of v1, /device:TPU:1, one launch (start us, length us, event | category | flops | bytes accessed | tf_op | source)
XLA Modules:
  0.0 75.4 jit_solution(11428821341920753414)
XLA Ops:
  0.0 0.0 copy-start.5
  0.0 0.0 copy-start.6
  0.0 0.7 copy-done.5
  0.7 0.0 copy-done.6
  0.7 0.0 copy-start
  0.7 1.1 %copy-done = bf16[48,48,128]{2,1,0:T(8,128)(2,1)S(1)} copy-done((bf16[48,48,128]{2,1,0:T(8,128)(2,1)S(1)}, bf16[48,48,128]{2,1,0:T(8,128)(2,1)}, u32[]{:S(2)}) %copy-start) | copy-done | bytes 589848
  1.7 0.0 copy-start.1
  1.7 0.8 %copy-done.1 = bf16[128,128]{1,0:T(8,128)(2,1)S(1)} copy-done((bf16[128,128]{1,0:T(8,128)(2,1)S(1)}, bf16[128,128]{1,0:T(8,128)(2,1)}, u32[]{:S(2)}) %copy-start.1) | copy-done | bytes 32792
  2.5 0.0 copy-start.2
  2.5 0.8 %copy-done.2 = bf16[128,128]{1,0:T(8,128)(2,1)S(1)} copy-done((bf16[128,128]{1,0:T(8,128)(2,1)S(1)}, bf16[128,128]{1,0:T(8,128)(2,1)}, u32[]{:S(2)}) %copy-start.2) | copy-done | bytes 32792
  3.3 0.0 copy-start.3
  3.3 0.8 %copy-done.3 = bf16[128,128]{1,0:T(8,128)(2,1)S(1)} copy-done((bf16[128,128]{1,0:T(8,128)(2,1)S(1)}, bf16[128,128]{1,0:T(8,128)(2,1)}, u32[]{:S(2)}) %copy-start.3) | copy-done | bytes 32792
  4.0 0.0 copy-start.4
  4.0 0.8 %copy-done.4 = bf16[128,128]{1,0:T(8,128)(2,1)S(1)} copy-done((bf16[128,128]{1,0:T(8,128)(2,1)S(1)}, bf16[128,128]{1,0:T(8,128)(2,1)}, u32[]{:S(2)}) %copy-start.4) | copy-done | bytes 32792
  4.8 69.8 %shard_map.73 = bf16[48,48,128]{2,1,0:T(8,128)(2,1)S(1)} custom-call(bf16[48,48,128]{2,1,0:T(8,128)(2,1)S(1)} %copy-done, f32[1,128]{1,0:T(1,128)S(1)} %bitcast.2, bf16[128,128]{1,0:T(8,128)(2,1)S(1)} %copy-done.1, bf16[128,128]{1,0:T(8,128)(2,1)S(1)} %copy-done.2, f32[1,128]{1,0:T(1,128)S(1)} %bitcast.3, bf16[128,128]{1,0:T(8,128)(2,1)S(1)} %copy-done.3, ...), custom_call_target="tpu_custom_call" | custom-call | tf_op jit(solution)/shard_map/pallas_call | solution.py:330
  74.6 0.8 %copy.9 = bf16[48,48,128]{2,1,0:T(8,128)(2,1)} copy(bf16[48,48,128]{2,1,0:T(8,128)(2,1)S(1)} %shard_map.73) | data formatting | bytes 1179648
Async XLA Ops:
  0.0 0.7 copy-start.5
  0.0 0.7 copy-start.6
  0.7 1.1 %copy-start = (bf16[48,48,128]{2,1,0:T(8,128)(2,1)S(1)}, bf16[48,48,128]{2,1,0:T(8,128)(2,1)}, u32[]{:S(2)}) copy-start(bf16[48,48,128]{2,1,0:T(8,128)(2,1)} %x_ref.1) | copy-start | bytes 1769476
  1.7 0.8 %copy-start.1 = (bf16[128,128]{1,0:T(8,128)(2,1)S(1)}, bf16[128,128]{1,0:T(8,128)(2,1)}, u32[]{:S(2)}) copy-start(bf16[128,128]{1,0:T(8,128)(2,1)} %left_w.1) | copy-start | bytes 98308
  2.5 0.8 %copy-start.2 = (bf16[128,128]{1,0:T(8,128)(2,1)S(1)}, bf16[128,128]{1,0:T(8,128)(2,1)}, u32[]{:S(2)}) copy-start(bf16[128,128]{1,0:T(8,128)(2,1)} %right_w.1) | copy-start | bytes 98308
  3.3 0.8 %copy-start.3 = (bf16[128,128]{1,0:T(8,128)(2,1)S(1)}, bf16[128,128]{1,0:T(8,128)(2,1)}, u32[]{:S(2)}) copy-start(bf16[128,128]{1,0:T(8,128)(2,1)} %out_w.1) | copy-start | bytes 98308
  4.0 0.8 %copy-start.4 = (bf16[128,128]{1,0:T(8,128)(2,1)S(1)}, bf16[128,128]{1,0:T(8,128)(2,1)}, u32[]{:S(2)}) copy-start(bf16[128,128]{1,0:T(8,128)(2,1)} %out_gate.1) | copy-start | bytes 98308

commit v2 on v0

v2 whole, which is shorter than its diff:
```python
import functools

import jax
import jax.numpy as jnp
from jax import lax
from jax.experimental import pallas as pl
from jax.experimental.pallas import tpu as pltpu
from jax.sharding import PartitionSpec as P

MESH = pl.DeviceIdType.MESH
NX, NY, NS = 4, 4, 16
BLK = 48
SUB = 16
NP = BLK // SUB
W = 128
KALL = BLK * NS


def unit_channels(values, channel_gain):
    centred = values - jnp.mean(values, axis=-1, keepdims=True)
    return (
        centred
        * lax.rsqrt(jnp.mean(centred * centred, axis=-1, keepdims=True) + 1e-05)
        * channel_gain
    )


def butterfly(slabs, first_stride):
    n = len(slabs)
    lane = lax.broadcasted_iota(jnp.int32, slabs[0].shape, 1)
    bit = 1
    while bit < n:
        stride = bit * first_stride
        low = (lane // stride) % 2 == 0
        out = list(slabs)
        for a in range(n):
            if a & bit:
                continue
            b = a | bit
            u, v = slabs[a], slabs[b]
            out[a] = jnp.where(low, u, pltpu.roll(v, stride, 1))
            out[b] = jnp.where(low, pltpu.roll(u, W - stride, 1), v)
        slabs = out
        bit *= 2
    return slabs


def kernel(
    x_hbm, in_gain_hbm, left_hbm, right_hbm, mid_gain_hbm, out_hbm, gate_hbm,
    o_ref,
    x_ref, in_gain, left_w, right_w, mid_gain, out_w, out_gate, ls,
    ready, gate, send_l, send_r, land_r, left_g, right_g, stage, middle, land_o,
    zs, zr, gs, gr, hs, hr, os_, or_,
):
    f, s = lax.axis_index("first"), lax.axis_index("second")
    y, x = f // NX, f % NX

    def dev(first, second):
        return {"first": first, "second": second}

    turned = s % 2

    def pick(straight, crossed):
        return straight + turned * (crossed - straight)

    slot = (pick(x, y), pick(y, x))

    def ring(which, step):
        along_x, along_y = y * NX + (x + step) % NX, (y + step) % NY * NX + x
        return pick(along_x, along_y) if which == 0 else pick(along_y, along_x)


    loads = [
        pltpu.make_async_copy(src, dst, ls.at[n])
        for n, (src, dst) in enumerate((
            (right_hbm, right_w), (in_gain_hbm, in_gain), (left_hbm, left_w),
            (x_hbm.at[pl.ds(0, SUB)], x_ref.at[pl.ds(0, SUB)]),
            (x_hbm.at[pl.ds(SUB, BLK - SUB)], x_ref.at[pl.ds(SUB, BLK - SUB)]),
            (gate_hbm, out_gate), (mid_gain_hbm, mid_gain), (out_hbm, out_w),
        ))
    ]
    for load in loads:
        load.start()

    barrier = pltpu.get_barrier_semaphore()

    def greet(first, second):
        pl.semaphore_signal(barrier, inc=1, device_id=dev(first, second), device_id_type=MESH)

    def greet_line(t, carry):
        greet(f, (s + t) % NS)
        return carry

    lax.fori_loop(1, NS, greet_line, 0)
    for step in (1, NX - 1):
        for which in (0, 1):
            greet(ring(which, step), s)
    greet(ring(0, 2), s)


    rows = lax.broadcasted_iota(jnp.int32, (W, W), 0)
    cols = lax.broadcasted_iota(jnp.int32, (W, W), 1)
    swap = (rows == (cols % 16) * 8 + cols // 16).astype(jnp.bfloat16)
    loads[0].wait()
    right_mix = jnp.dot(
        right_w[...], swap, preferred_element_type=jnp.float32
    ).astype(jnp.bfloat16)

    def line_copy(t, p, which):
        h = (t // 2 + 1) // 2 * (2 * ((t // 2) % 2) - 1)
        to = ((s // 2 + h + 8) % 8) * 2 + (s + t) % 2
        if which == 0:
            there = x + to % 2 * (y - x)
            src, dst = send_l.at[to, p], left_g.at[p, there, pl.ds(pl.multiple_of(s * BLK, BLK), BLK)]
        else:
            src, dst = send_r.at[to, p], land_r.at[p, pl.ds(pl.multiple_of(s * BLK, BLK), BLK)]
        return pltpu.make_async_remote_copy(
            src_ref=src, dst_ref=dst, send_sem=zs.at[p, which], recv_sem=zr.at[p, which],
            device_id=dev(f, to), device_id_type=MESH,
        )

    def line_local(p, which):
        if which == 0:
            src, dst = send_l.at[s, p], left_g.at[p, slot[0], pl.ds(pl.multiple_of(s * BLK, BLK), BLK)]
        else:
            src, dst = send_r.at[s, p], land_r.at[p, pl.ds(pl.multiple_of(s * BLK, BLK), BLK)]
        return pltpu.make_async_copy(src, dst, zr.at[p, which])

    def factor_piece(p):
        at = pl.multiple_of(p * SUB, SUB)
        values = x_ref[pl.ds(at, SUB)].reshape(SUB * BLK, W).astype(jnp.float32)
        r = unit_channels(values, in_gain[...]).astype(jnp.bfloat16)
        ready[pl.ds(at, SUB)] = r.reshape(SUB, BLK, W)
        for which, weight, stride, buf in ((0, left_w[...], 8, send_l), (1, right_mix, 1, send_r)):
            full = jnp.dot(r, weight, preferred_element_type=jnp.float32)
            full = full.astype(jnp.bfloat16).reshape(SUB, BLK, W)
            slabs = butterfly([full[i] for i in range(SUB)], stride)
            for i in range(SUB):
                buf[i, p] = slabs[i]

    def send_piece(which, p):
        line_local(p, which).start()

        def go(t, carry):
            line_copy(t, p, which).start()
            return carry

        lax.fori_loop(1, NS, go, 0)

    def gate_rows(i, carry):
        at = pl.multiple_of(i * SUB, SUB)
        r = ready[pl.ds(at, SUB)].reshape(SUB * BLK, W)
        g = jax.nn.sigmoid(jnp.dot(r, out_gate[...], preferred_element_type=jnp.float32))
        gate[pl.ds(at, SUB)] = g.reshape(SUB, BLK, W)
        return carry

    def piece(p, carry):
        factor_piece(p)
        return carry

    for load in loads[1:]:
        load.wait()
    with jax.named_scope("factor"):
        lax.fori_loop(0, NP, piece, 0)
    with jax.named_scope("gate"):
        lax.fori_loop(0, NP, gate_rows, 0)
    with jax.named_scope("barrier"):
        pl.semaphore_wait(barrier, (NS - 1) + 5)
    with jax.named_scope("send"):
        for p in range(NP):
            for which in (0, 1):
                send_piece(which, p)

    def ring_copy(which, p, block, part, step, sem):
        buf = (left_g, right_g)[which]
        size = buf.shape[2] // 2
        ref = buf.at[p, block, pl.ds(part * size, size)]
        return pltpu.make_async_remote_copy(
            src_ref=ref, dst_ref=ref, send_sem=gs.at[p, which], recv_sem=gr.at[p, which, sem],
            device_id=dev(ring(which, step), s), device_id_type=MESH,
        )

    def ring_wait(which, p, blocks, part, sem):
        buf = (left_g, right_g)[which]
        size = buf.shape[2] // 2
        ref = buf.at[p, pl.ds(0, blocks), pl.ds(part * size, size)]
        if blocks > 1:
            ref = buf.at[p, pl.ds(0, blocks)]
        pltpu.make_async_copy(ref, ref, sem).wait()

    def gather(which, p):
        with jax.named_scope(f"line{which}{p}"):
            ref = left_g.at[p, slot[0]] if which == 0 else land_r.at[p]
            pltpu.make_async_copy(ref, ref, zr.at[p, which]).wait()
        if which == 1:
            with jax.named_scope(f"turn{p}"):
                right_g[p, slot[1]] = jnp.transpose(land_r[p])
        me = slot[which]
        ring_copy(which, p, me, 0, 1, 0).start()
        ring_copy(which, p, me, 1, NX - 1, 1).start()
        ring_copy(which, p, me, 1, 1, 2).start()
        ring_copy(which, p, me, 0, NX - 1, 2).start()

    def pass_on(which, p):
        with jax.named_scope(f"pass{which}{p}"):
            ring_wait(which, p, 1, 0, gr.at[p, which, 0])
            ring_copy(which, p, (slot[which] + NX - 1) % NX, 0, 1, 2).start()
            ring_wait(which, p, 1, 1, gr.at[p, which, 1])
            ring_copy(which, p, (slot[which] + 1) % NX, 1, NX - 1, 2).start()

    def gathered(which, p):
        with jax.named_scope(f"gathered{which}{p}"):
            ring_wait(which, p, 2, 0, gr.at[p, which, 2])

    lane_channel = lax.broadcasted_iota(jnp.int32, (SUB, W), 1) % 8

    def product(a, b):
        with jax.named_scope(f"prod{a}{b}"):
            right = right_g[b].reshape(NY * W, KALL)
            for h in range(2):
                left = jnp.concatenate([left_g[a, 2 * h], left_g[a, 2 * h + 1]], axis=1)
                full = jnp.dot(right, left, preferred_element_type=jnp.float32)
                for v in range(NY):
                    for u in range(2):
                        tile = full[v * W : (v + 1) * W, u * W : (u + 1) * W]
                        res = tile[:SUB]
                        for d in range(1, 8):
                            res = jnp.where(lane_channel == d, tile[d * SUB : (d + 1) * SUB], res)
                        res = (res * KALL ** (-0.5)).astype(jnp.bfloat16)
                        stage[2 * h + u, b, a, v] = res

    def hop_copy(a, b, step):
        to = (slot[0] + step) % NX
        return pltpu.make_async_remote_copy(
            src_ref=stage.at[to, b, a], dst_ref=middle.at[slot[0], b, a],
            send_sem=hs.at[b, a], recv_sem=hr.at[b, a],
            device_id=dev(ring(0, step), s), device_id_type=MESH,
        )

    def hop(a, b):
        for step in (2, 1, 3):
            hop_copy(a, b, step).start()
        middle[slot[0], b, a] = stage[slot[0], b, a]

    def spread(a, b):
        with jax.named_scope(f"hopwait{a}{b}"):
            ref = middle.at[pl.ds(0, 3), b, a]
            pltpu.make_async_copy(ref, ref, hr.at[b, a]).wait()

        def source(to):
            w, v = pick(to % NX, to // NX), pick(to // NX, to % NX)
            return middle.at[w, b, a, v]

        def go(t, carry):
            h = (t // 2 + 1) // 2 * (2 * ((t // 2) % 2) - 1)
            to = ((s // 2 + h + 8) % 8) * 2 + (s + t) % 2
            pltpu.make_async_remote_copy(
                src_ref=source(to), dst_ref=land_o.at[s, b, a],
                send_sem=os_.at[b, a], recv_sem=or_.at[b, a],
                device_id=dev(f, to), device_id_type=MESH,
            ).start()
            return carry

        with jax.named_scope(f"spread{a}{b}"):
            lax.fori_loop(1, NS, go, 0)
            pltpu.make_async_copy(source(s), land_o.at[s, b, a], or_.at[b, a]).start()

    def arrived(a, b):
        ref = land_o.at[:, b, a]
        with jax.named_scope(f"arrive{a}{b}"):
            pltpu.make_async_copy(ref, ref, or_.at[b, a]).wait()

    def finish(a, b):
        with jax.named_scope(f"fin{a}{b}"):
            at = pl.ds(b * SUB, SUB)
            rows_ = pl.ds(a * SUB, SUB)
            slabs = butterfly([land_o[i, b, a] for i in range(NS)], 8)
            mixed = jnp.concatenate(slabs, axis=0).astype(jnp.float32)
            scaled = unit_channels(mixed, mid_gain[...]).astype(jnp.bfloat16)
            res = jnp.dot(scaled, out_w[...], preferred_element_type=jnp.float32)
            o_ref[rows_, at] = (res.reshape(SUB, SUB, W) * gate[rows_, at]).astype(jnp.bfloat16)

    def make(a, b):
        product(a, b)
        hop(a, b)

    def end(a, b):
        arrived(a, b)
        finish(a, b)

    left, right = 0, 1
    gather(left, 0)
    gather(right, 0)
    pass_on(left, 0)
    gather(left, 1)
    pass_on(right, 0)
    gathered(left, 0)
    gather(right, 1)
    pass_on(left, 1)
    gathered(right, 0)
    make(0, 0)
    gather(left, 2)
    pass_on(right, 1)
    gathered(left, 1)
    make(1, 0)
    gather(right, 2)
    spread(0, 0)
    pass_on(left, 2)
    gathered(right, 1)
    make(0, 1)
    pass_on(right, 2)
    make(1, 1)
    spread(1, 0)
    gathered(left, 2)
    make(2, 0)
    spread(0, 1)
    make(2, 1)
    spread(1, 1)
    gathered(right, 2)
    make(0, 2)
    spread(2, 0)
    make(1, 2)
    spread(2, 1)
    make(2, 2)
    end(0, 0)
    spread(0, 2)
    end(1, 0)
    spread(1, 2)
    spread(2, 2)
    end(0, 1)
    end(1, 1)
    end(2, 0)
    end(2, 1)
    end(0, 2)
    end(1, 2)
    end(2, 2)

    for p in range(NP):
        for which in (0, 1):
            buf = (send_l, send_r)[which]
            ref = buf.at[pl.ds(0, NS - 1), p]
            pltpu.make_async_copy(ref, ref, zs.at[p, which]).wait()
            ring_wait(which, p, 3, 0, gs.at[p, which])
    for b in range(NP):
        for a in range(NP):
            ref = middle.at[pl.ds(0, 3), b, a]
            pltpu.make_async_copy(ref, ref, hs.at[b, a]).wait()
            ref = land_o.at[pl.ds(0, NS - 1), b, a]
            pltpu.make_async_copy(ref, ref, os_.at[b, a]).wait()


def per_device(pair_state, in_gain, left_weight, right_weight, mid_gain, out_weight, out_gate):
    bf = jnp.bfloat16
    vmem = pl.BlockSpec(memory_space=pltpu.VMEM)
    return pl.pallas_call(
        kernel,
        out_shape=jax.ShapeDtypeStruct((BLK, BLK, W), bf),
        in_specs=[pl.BlockSpec(memory_space=pltpu.HBM)] * 7,
        out_specs=vmem,
        scratch_shapes=[
            pltpu.VMEM((BLK, BLK, W), bf),
            pltpu.VMEM((1, W), jnp.float32),
            pltpu.VMEM((W, W), bf),
            pltpu.VMEM((W, W), bf),
            pltpu.VMEM((1, W), jnp.float32),
            pltpu.VMEM((W, W), bf),
            pltpu.VMEM((W, W), bf),
            pltpu.SemaphoreType.DMA((8,)),
            pltpu.VMEM((BLK, BLK, W), bf),
            pltpu.VMEM((BLK, BLK, W), jnp.float32),
            pltpu.VMEM((NS, NP, BLK, W), bf),
            pltpu.VMEM((NS, NP, BLK, W), bf),
            pltpu.VMEM((NP, KALL, W), bf),
            pltpu.VMEM((NP, NX, KALL, W), bf),
            pltpu.VMEM((NP, NY, W, KALL), bf),
            pltpu.VMEM((NX, NP, NP, NY, SUB, W), bf),
            pltpu.VMEM((NX, NP, NP, NY, SUB, W), bf),
            pltpu.VMEM((NS, NP, NP, SUB, W), bf),
            pltpu.SemaphoreType.DMA((NP, 2)),
            pltpu.SemaphoreType.DMA((NP, 2)),
            pltpu.SemaphoreType.DMA((NP, 2)),
            pltpu.SemaphoreType.DMA((NP, 2, 3)),
            pltpu.SemaphoreType.DMA((NP, NP)),
            pltpu.SemaphoreType.DMA((NP, NP)),
            pltpu.SemaphoreType.DMA((NP, NP)),
            pltpu.SemaphoreType.DMA((NP, NP)),
        ],
        compiler_params=pltpu.CompilerParams(
            collective_id=0, has_side_effects=True, vmem_limit_bytes=50_331_648
        ),
    )(*(pltpu.with_memory_space_constraint(v, pltpu.HBM) for v in (pair_state, in_gain.reshape(1, W), left_weight, right_weight, mid_gain.reshape(1, W), out_weight, out_gate)))


def solution(mesh):
    in_specs = (P("first", "second", None), P(), P(), P(), P(), P(), P())
    out_specs = P("first", "second", None)
    return jax.shard_map(
        per_device, mesh=mesh, in_specs=in_specs, out_specs=out_specs, check_vma=False
    )
```

time: 181 us -> 64.9 us (0.36)
  waiting for transfers between devices: 64.7 us -> 0 us
  Pallas kernels: 0 us -> 63.9 us
  blocking collectives: 50.2 us -> 0 us
  local copies, waits for them, and re-layouts: 27.7 us -> 0.82 us
  between operations: 13.7 us -> 0.01 us
  matrix products: 9.99 us -> 0 us
  starting transfers between devices: 7.95 us -> 0 us
  other arithmetic: 6.45 us -> 0 us
    pallas_call x0 -> x1, Pallas kernels: none -> 63.9 us  [per_device(): pl.pallas_call(kernel, out_shape=jax.ShapeDtypeStruct((BLK, BLK, W), bf),...]
    all_to_all x2 -> x0, blocking collectives: 50.2 us -> none  [the longest x1 28.4 us: per_device(): lax.all_to_all(right, 'second', split_axis=2, concat_axis=1, tiled=True)]
    all_gather x1 -> x0, waiting for transfers between devices: 47.9 us -> none  [per_device(): strip = meet(lax.all_gather(right_lines, 'first', axis=0, tiled=True))]
    all_to_all x1 -> x0, waiting for transfers between devices: 16.8 us -> none  [per_device(): lax.all_to_all(strip, 'second', split_axis=1, concat_axis=2, tiled=True)]
    unnamed x26 -> x1, local copies, waits for them, and re-layouts: 14.7 us -> 0.82 us
    dot_general x5 -> x0, matrix products: 9.99 us -> none  [the longest x1 6.53 us: meet(): jnp.einsum('ikd,jkd->ijd', left_lines, piece, preferred_element_type=jnp....]
    all_to_all x1 -> x0, starting transfers between devices: 7.95 us -> none  [per_device(): lax.all_to_all(strip, 'second', split_axis=1, concat_axis=2, tiled=True)]
    convert_element_type x4 -> x0, local copies, waits for them, and re-layouts: 7.08 us -> none  [the longest x1 4.06 us: finish_pair(): mixed.astype(jnp.float32)]
  transfers between devices with their start and end apart: 2 -> 0, of which waited for: 2 -> 0; matrix products, arithmetic and copies ran while one was open for 4% -> 0% of each run, Pallas kernels for 0% -> 0%
where the time goes in v2:
time: 64.9 us; the launch traced here: 64.8 us
  Pallas kernels  63.9 us (98%)
  local copies, waits for them, and re-layouts  0.82 us (1%)
    pallas_call x1, Pallas kernels, per_device(): pl.pallas_call(kernel, out_shape=jax.ShapeDtypeStruct((BLK, BLK, W), bf),...  63.9 us

profile of v2, /device:TPU:1, one launch (start us, length us, event | category | flops | bytes accessed | tf_op | source)
XLA Modules:
  0.0 64.8 jit_solution(1639519927864536578)
XLA Ops:
  0.0 63.9 %shard_map.73 = bf16[48,48,128]{2,1,0:T(8,128)(2,1)S(1)} custom-call(bf16[48,48,128]{2,1,0:T(8,128)(2,1)} %x_hbm.1, f32[1,128]{1,0:T(1,128)} %bitcast.2, bf16[128,128]{1,0:T(8,128)(2,1)} %left_hbm.1, bf16[128,128]{1,0:T(8,128)(2,1)} %right_hbm.1, f32[1,128]{1,0:T(1,128)} %bitcast.3, bf16[128,128]{1,0:T(8,128)(2,1)} %out_hbm.1, bf16[128,128]{1,0:T(8,128)(2,1)} %gate_hbm.1), custom_call_target="tpu_custom_call" | custom-call | tf_op jit(solution)/shard_map/pallas_call | solution.py:355
  63.9 0.8 %copy.9 = bf16[48,48,128]{2,1,0:T(8,128)(2,1)} copy(bf16[48,48,128]{2,1,0:T(8,128)(2,1)S(1)} %shard_map.73) | data formatting | bytes 1179648

commit v3 on v2

--- a/solution.py
+++ b/solution.py
@@ -14,6 +14,20 @@
 NP = BLK // SUB
 W = 128
 KALL = BLK * NS
+NQ = BLK // SUB
+PART = NS * SUB
+UNITS = (
+    (0, 0, 0, 3),
+    (1, 0, 0, 3),
+    (0, 1, 0, 3),
+    (1, 1, 0, 3),
+    (0, 2, 0, 3),
+    (1, 2, 0, 2),
+    (1, 2, 2, 3),
+)
+
+
+PEERS = tuple((h, other) for other in (0, 1) for h in (4, 3, -3, 2, -2, 1, -1, 0) if (h, other) != (0, 0))
 
 
 def unit_channels(values, channel_gain):
@@ -106,46 +120,55 @@
         right_w[...], swap, preferred_element_type=jnp.float32
     ).astype(jnp.bfloat16)
 
-    def line_copy(t, p, which):
-        h = (t // 2 + 1) // 2 * (2 * ((t // 2) % 2) - 1)
-        to = ((s // 2 + h + 8) % 8) * 2 + (s + t) % 2
+    def line_peer(t):
+        h, other = PEERS[t]
+        return ((s // 2 + h + 8) % 8) * 2 + (s + other) % 2
+
+    def for_peers(go):
+        for t in range(NS - 1):
+            go(t, 0)
+
+    rows_s = pl.ds(pl.multiple_of(s * SUB, SUB), SUB)
+
+    def line_ends(n, to):
+        which, p, q0, q1 = UNITS[n]
+        parts = pl.ds(q0, q1 - q0)
         if which == 0:
             there = x + to % 2 * (y - x)
-            src, dst = send_l.at[to, p], left_g.at[p, there, pl.ds(pl.multiple_of(s * BLK, BLK), BLK)]
-        else:
-            src, dst = send_r.at[to, p], land_r.at[p, pl.ds(pl.multiple_of(s * BLK, BLK), BLK)]
+            return send_l.at[to, p, parts], left_g.at[p, there, parts, rows_s]
+        return send_r.at[to, p, parts], land_r.at[p, parts, rows_s]
+
+    def line_copy(n, t):
+        to = line_peer(t)
+        src, dst = line_ends(n, to)
         return pltpu.make_async_remote_copy(
-            src_ref=src, dst_ref=dst, send_sem=zs.at[p, which], recv_sem=zr.at[p, which],
+            src_ref=src, dst_ref=dst, send_sem=zs.at[n], recv_sem=zr.at[n],
             device_id=dev(f, to), device_id_type=MESH,
         )
 
-    def line_local(p, which):
-        if which == 0:
-            src, dst = send_l.at[s, p], left_g.at[p, slot[0], pl.ds(pl.multiple_of(s * BLK, BLK), BLK)]
-        else:
-            src, dst = send_r.at[s, p], land_r.at[p, pl.ds(pl.multiple_of(s * BLK, BLK), BLK)]
-        return pltpu.make_async_copy(src, dst, zr.at[p, which])
-
-    def factor_piece(p):
-        at = pl.multiple_of(p * SUB, SUB)
-        values = x_ref[pl.ds(at, SUB)].reshape(SUB * BLK, W).astype(jnp.float32)
-        r = unit_channels(values, in_gain[...]).astype(jnp.bfloat16)
-        ready[pl.ds(at, SUB)] = r.reshape(SUB, BLK, W)
-        for which, weight, stride, buf in ((0, left_w[...], 8, send_l), (1, right_mix, 1, send_r)):
-            full = jnp.dot(r, weight, preferred_element_type=jnp.float32)
-            full = full.astype(jnp.bfloat16).reshape(SUB, BLK, W)
-            slabs = butterfly([full[i] for i in range(SUB)], stride)
-            for i in range(SUB):
-                buf[i, p] = slabs[i]
-
-    def send_piece(which, p):
-        line_local(p, which).start()
+    def norm_piece(p):
+        at = pl.ds(p * SUB, SUB)
+        values = x_ref[at].reshape(SUB * BLK, W).astype(jnp.float32)
+        ready[at] = unit_channels(values, in_gain[...]).astype(jnp.bfloat16).reshape(SUB, BLK, W)
+
+    def factor_piece(which, p):
+        r = ready[pl.ds(p * SUB, SUB)].reshape(SUB * BLK, W)
+        weight, stride, buf = ((left_w[...], 8, send_l), (right_mix, 1, send_r))[which]
+        full = jnp.dot(r, weight, preferred_element_type=jnp.float32)
+        full = full.astype(jnp.bfloat16).reshape(SUB, BLK, W)
+        slabs = butterfly([full[i] for i in range(SUB)], stride)
+        for i in range(SUB):
+            buf[i, p] = slabs[i].reshape(NQ, SUB, W)
+
+    def send(n):
+        src, dst = line_ends(n, s)
+        pltpu.make_async_copy(src, dst, zr.at[n]).start()
 
         def go(t, carry):
-            line_copy(t, p, which).start()
+            line_copy(n, t).start()
             return carry
 
-        lax.fori_loop(1, NS, go, 0)
+        for_peers(go)
 
     def gate_rows(i, carry):
         at = pl.multiple_of(i * SUB, SUB)
@@ -154,63 +177,75 @@
         gate[pl.ds(at, SUB)] = g.reshape(SUB, BLK, W)
         return carry
 
-    def piece(p, carry):
-        factor_piece(p)
-        return carry
-
-    for load in loads[1:]:
-        load.wait()
+    loads[1].wait()
+    loads[2].wait()
+    loads[3].wait()
     with jax.named_scope("factor"):
-        lax.fori_loop(0, NP, piece, 0)
-    with jax.named_scope("gate"):
-        lax.fori_loop(0, NP, gate_rows, 0)
+        norm_piece(0)
+        factor_piece(0, 0)
     with jax.named_scope("barrier"):
         pl.semaphore_wait(barrier, (NS - 1) + 5)
     with jax.named_scope("send"):
-        for p in range(NP):
-            for which in (0, 1):
-                send_piece(which, p)
-
-    def ring_copy(which, p, block, part, step, sem):
-        buf = (left_g, right_g)[which]
-        size = buf.shape[2] // 2
-        ref = buf.at[p, block, pl.ds(part * size, size)]
+        done = {(0, 0)}
+        for n, (which, p, q0, q1) in enumerate(UNITS):
+            if (which, p) not in done:
+                if (1 - which, p) not in done:
+                    if p == 1:
+                        loads[4].wait()
+                    norm_piece(p)
+                factor_piece(which, p)
+                done.add((which, p))
+            send(n)
+    for load in loads[5:]:
+        load.wait()
+    with jax.named_scope("gate"):
+        lax.fori_loop(0, NP, gate_rows, 0)
+
+    def ring_part(n, blocks, half=None):
+        which, p, q0, q1 = UNITS[n]
+        parts = q1 - q0
+        if which == 0:
+            rows_ = pl.ds(0, PART) if half is None else pl.ds(half * (PART // 2), PART // 2)
+            return left_g.at[p, blocks, pl.ds(q0, parts), rows_]
+        rows_ = pl.ds(0, W) if half is None else pl.ds(half * (W // 2), W // 2)
+        return right_g.at[p, blocks, rows_, pl.ds(q0 * PART, parts * PART)]
+
+    def ring_copy(n, block, half, step, sem):
+        ref = ring_part(n, block, half)
         return pltpu.make_async_remote_copy(
-            src_ref=ref, dst_ref=ref, send_sem=gs.at[p, which], recv_sem=gr.at[p, which, sem],
-            device_id=dev(ring(which, step), s), device_id_type=MESH,
+            src_ref=ref, dst_ref=ref, send_sem=gs.at[n], recv_sem=gr.at[n, sem],
+            device_id=dev(ring(UNITS[n][0], step), s), device_id_type=MESH,
         )
 
-    def ring_wait(which, p, blocks, part, sem):
-        buf = (left_g, right_g)[which]
-        size = buf.shape[2] // 2
-        ref = buf.at[p, pl.ds(0, blocks), pl.ds(part * size, size)]
-        if blocks > 1:
-            ref = buf.at[p, pl.ds(0, blocks)]
+    def wait_for(ref, sem):
         pltpu.make_async_copy(ref, ref, sem).wait()
 
-    def gather(which, p):
-        with jax.named_scope(f"line{which}{p}"):
-            ref = left_g.at[p, slot[0]] if which == 0 else land_r.at[p]
-            pltpu.make_async_copy(ref, ref, zr.at[p, which]).wait()
+    def gather(n):
+        which, p, q0, q1 = UNITS[n]
+        parts = pl.ds(q0, q1 - q0)
+        with jax.named_scope(f"line{n}"):
+            wait_for(left_g.at[p, slot[0], parts] if which == 0 else land_r.at[p, parts], zr.at[n])
         if which == 1:
-            with jax.named_scope(f"turn{p}"):
-                right_g[p, slot[1]] = jnp.transpose(land_r[p])
+            with jax.named_scope(f"turn{n}"):
+                block = land_r[p, q0:q1].reshape((q1 - q0) * PART, W)
+                right_g[p, slot[1], :, q0 * PART : q1 * PART] = jnp.transpose(block)
         me = slot[which]
-        ring_copy(which, p, me, 0, 1, 0).start()
-        ring_copy(which, p, me, 1, NX - 1, 1).start()
-        ring_copy(which, p, me, 1, 1, 2).start()
-        ring_copy(which, p, me, 0, NX - 1, 2).start()
-
-    def pass_on(which, p):
-        with jax.named_scope(f"pass{which}{p}"):
-            ring_wait(which, p, 1, 0, gr.at[p, which, 0])
-            ring_copy(which, p, (slot[which] + NX - 1) % NX, 0, 1, 2).start()
-            ring_wait(which, p, 1, 1, gr.at[p, which, 1])
-            ring_copy(which, p, (slot[which] + 1) % NX, 1, NX - 1, 2).start()
-
-    def gathered(which, p):
-        with jax.named_scope(f"gathered{which}{p}"):
-            ring_wait(which, p, 2, 0, gr.at[p, which, 2])
+        ring_copy(n, me, 0, 1, 0).start()
+        ring_copy(n, me, 1, NX - 1, 1).start()
+        ring_copy(n, me, 1, 1, 2).start()
+        ring_copy(n, me, 0, NX - 1, 2).start()
+
+    def pass_on(n):
+        me = slot[UNITS[n][0]]
+        with jax.named_scope(f"pass{n}"):
+            wait_for(ring_part(n, 0, 0), gr.at[n, 0])
+            ring_copy(n, (me + NX - 1) % NX, 0, 1, 2).start()
+            wait_for(ring_part(n, 0, 1), gr.at[n, 1])
+            ring_copy(n, (me + 1) % NX, 1, NX - 1, 2).start()
+
+    def gathered(n):
+        with jax.named_scope(f"gathered{n}"):
+            wait_for(ring_part(n, pl.ds(0, 2)), gr.at[n, 2])
 
     lane_channel = lax.broadcasted_iota(jnp.int32, (SUB, W), 1) % 8
 
@@ -218,7 +253,9 @@
         with jax.named_scope(f"prod{a}{b}"):
             right = right_g[b].reshape(NY * W, KALL)
             for h in range(2):
-                left = jnp.concatenate([left_g[a, 2 * h], left_g[a, 2 * h + 1]], axis=1)
+                left = jnp.concatenate(
+                    [left_g[a, 2 * h + u].reshape(KALL, W) for u in range(2)], axis=1
+                )
                 full = jnp.dot(right, left, preferred_element_type=jnp.float32)
                 for v in range(NY):
                     for u in range(2):
@@ -252,8 +289,7 @@
             return middle.at[w, b, a, v]
 
         def go(t, carry):
-            h = (t // 2 + 1) // 2 * (2 * ((t // 2) % 2) - 1)
-            to = ((s // 2 + h + 8) % 8) * 2 + (s + t) % 2
+            to = line_peer(t)
             pltpu.make_async_remote_copy(
                 src_ref=source(to), dst_ref=land_o.at[s, b, a],
                 send_sem=os_.at[b, a], recv_sem=or_.at[b, a],
@@ -262,7 +298,7 @@
             return carry
 
         with jax.named_scope(f"spread{a}{b}"):
-            lax.fori_loop(1, NS, go, 0)
+            for_peers(go)
             pltpu.make_async_copy(source(s), land_o.at[s, b, a], or_.at[b, a]).start()
 
     def arrived(a, b):
@@ -288,65 +324,68 @@
         arrived(a, b)
         finish(a, b)
 
-    left, right = 0, 1
-    gather(left, 0)
-    gather(right, 0)
-    pass_on(left, 0)
-    gather(left, 1)
-    pass_on(right, 0)
-    gathered(left, 0)
-    gather(right, 1)
-    pass_on(left, 1)
-    gathered(right, 0)
+    def drain_tiles(tiles):
+        for a, b in tiles:
+            wait_for(middle.at[pl.ds(0, 3), b, a], hs.at[b, a])
+            wait_for(land_o.at[pl.ds(0, NS - 1), b, a], os_.at[b, a])
+
+    def drain():
+        for n, (which, p, q0, q1) in enumerate(UNITS):
+            wait_for((send_l, send_r)[which].at[pl.ds(0, NS - 1), p, pl.ds(q0, q1 - q0)], zs.at[n])
+            wait_for(ring_part(n, pl.ds(0, 3)), gs.at[n])
+        drain_tiles(((0, 0), (1, 0), (0, 1), (1, 1), (2, 0)))
+
+    gather(0)
+    gather(1)
+    pass_on(0)
+    gather(2)
+    pass_on(1)
+    gathered(0)
+    gather(3)
+    pass_on(2)
+    gathered(1)
     make(0, 0)
-    gather(left, 2)
-    pass_on(right, 1)
-    gathered(left, 1)
+    gather(4)
+    pass_on(3)
+    gathered(2)
     make(1, 0)
-    gather(right, 2)
+    gather(5)
     spread(0, 0)
-    pass_on(left, 2)
-    gathered(right, 1)
+    gather(6)
+    pass_on(4)
+    gathered(3)
     make(0, 1)
-    pass_on(right, 2)
+    pass_on(5)
     make(1, 1)
     spread(1, 0)
-    gathered(left, 2)
+    pass_on(6)
+    gathered(4)
     make(2, 0)
     spread(0, 1)
     make(2, 1)
     spread(1, 1)
-    gathered(right, 2)
+    gathered(5)
+    gathered(6)
     make(0, 2)
+    make(1, 2)
+    make(2, 2)
     spread(2, 0)
-    make(1, 2)
     spread(2, 1)
-    make(2, 2)
+    spread(0, 2)
     end(0, 0)
-    spread(0, 2)
+    spread(1, 2)
     end(1, 0)
-    spread(1, 2)
     spread(2, 2)
     end(0, 1)
     end(1, 1)
     end(2, 0)
     end(2, 1)
+    drain()
     end(0, 2)
     end(1, 2)
     end(2, 2)
 
-    for p in range(NP):
-        for which in (0, 1):
-            buf = (send_l, send_r)[which]
-            ref = buf.at[pl.ds(0, NS - 1), p]
-            pltpu.make_async_copy(ref, ref, zs.at[p, which]).wait()
-            ring_wait(which, p, 3, 0, gs.at[p, which])
-    for b in range(NP):
-        for a in range(NP):
-            ref = middle.at[pl.ds(0, 3), b, a]
-            pltpu.make_async_copy(ref, ref, hs.at[b, a]).wait()
-            ref = land_o.at[pl.ds(0, NS - 1), b, a]
-            pltpu.make_async_copy(ref, ref, os_.at[b, a]).wait()
+    drain_tiles(((2, 1), (0, 2), (1, 2), (2, 2)))
 
 
 def per_device(pair_state, in_gain, left_weight, right_weight, mid_gain, out_weight, out_gate):
@@ -368,18 +407,18 @@
             pltpu.SemaphoreType.DMA((8,)),
             pltpu.VMEM((BLK, BLK, W), bf),
             pltpu.VMEM((BLK, BLK, W), jnp.float32),
-            pltpu.VMEM((NS, NP, BLK, W), bf),
-            pltpu.VMEM((NS, NP, BLK, W), bf),
-            pltpu.VMEM((NP, KALL, W), bf),
-            pltpu.VMEM((NP, NX, KALL, W), bf),
+            pltpu.VMEM((NS, NP, NQ, SUB, W), bf),
+            pltpu.VMEM((NS, NP, NQ, SUB, W), bf),
+            pltpu.VMEM((NP, NQ, PART, W), bf),
+            pltpu.VMEM((NP, NX, NQ, PART, W), bf),
             pltpu.VMEM((NP, NY, W, KALL), bf),
             pltpu.VMEM((NX, NP, NP, NY, SUB, W), bf),
             pltpu.VMEM((NX, NP, NP, NY, SUB, W), bf),
             pltpu.VMEM((NS, NP, NP, SUB, W), bf),
-            pltpu.SemaphoreType.DMA((NP, 2)),
-            pltpu.SemaphoreType.DMA((NP, 2)),
-            pltpu.SemaphoreType.DMA((NP, 2)),
-            pltpu.SemaphoreType.DMA((NP, 2, 3)),
+            pltpu.SemaphoreType.DMA((len(UNITS),)),
+            pltpu.SemaphoreType.DMA((len(UNITS),)),
+            pltpu.SemaphoreType.DMA((len(UNITS),)),
+            pltpu.SemaphoreType.DMA((len(UNITS), 3)),
             pltpu.SemaphoreType.DMA((NP, NP)),
             pltpu.SemaphoreType.DMA((NP, NP)),
             pltpu.SemaphoreType.DMA((NP, NP)),

time: 64.9 us -> 60.5 us (0.932)
  Pallas kernels: 63.9 us -> 59.6 us
    pallas_call x1, Pallas kernels: 63.9 us -> 59.6 us  [per_device(): pl.pallas_call(kernel, out_shape=jax.ShapeDtypeStruct((BLK, BLK, W), bf),...]
where the time goes in v3:
time: 60.5 us
  Pallas kernels  59.6 us (99%)
  local copies, waits for them, and re-layouts  0.82 us (1%)
    pallas_call x1, Pallas kernels, per_device(): pl.pallas_call(kernel, out_shape=jax.ShapeDtypeStruct((BLK, BLK, W), bf),...  59.6 us

profile of v3, /device:TPU:1, one launch (start us, length us, event | category | flops | bytes accessed | tf_op | source)
XLA Modules:
  0.0 60.5 jit_solution(489888816494594951)
XLA Ops:
  0.0 59.6 %shard_map.73 = bf16[48,48,128]{2,1,0:T(8,128)(2,1)S(1)} custom-call(bf16[48,48,128]{2,1,0:T(8,128)(2,1)} %x_hbm.1, f32[1,128]{1,0:T(1,128)} %bitcast.2, bf16[128,128]{1,0:T(8,128)(2,1)} %left_hbm.1, bf16[128,128]{1,0:T(8,128)(2,1)} %right_hbm.1, f32[1,128]{1,0:T(1,128)} %bitcast.3, bf16[128,128]{1,0:T(8,128)(2,1)} %out_hbm.1, bf16[128,128]{1,0:T(8,128)(2,1)} %gate_hbm.1), custom_call_target="tpu_custom_call" | custom-call | tf_op jit(solution)/shard_map/pallas_call | solution.py:394
  59.6 0.8 %copy.9 = bf16[48,48,128]{2,1,0:T(8,128)(2,1)} copy(bf16[48,48,128]{2,1,0:T(8,128)(2,1)S(1)} %shard_map.73) | data formatting | bytes 1179648

commit v4 on v3

--- a/solution.py
+++ b/solution.py
@@ -28,6 +28,9 @@
 
 
 PEERS = tuple((h, other) for other in (0, 1) for h in (4, 3, -3, 2, -2, 1, -1, 0) if (h, other) != (0, 0))
+
+
+AHEAD = (2, 1, 3)
 
 
 def unit_channels(values, channel_gain):
@@ -277,52 +280,68 @@
     def hop(a, b):
         for step in (2, 1, 3):
             hop_copy(a, b, step).start()
-        middle[slot[0], b, a] = stage[slot[0], b, a]
+        spread_from(0, a, b)
+
+    group, place = pick(s % NX, s // NX), pick(s // NX, s % NX)
+
+    def spread_from(ahead, a, b):
+        w = (slot[0] + ahead) % NX
+
+        for k in (1, 2, 3, 0):
+            v = (place + k) % NY
+            to = pick(v * NX + w, w * NX + v)
+            src, dst = (stage.at[w, b, a, v] if ahead == 0 else middle.at[w, b, a, v]), land_o.at[s, b, a]
+
+            def far(src=src, dst=dst, to=to):
+                pltpu.make_async_remote_copy(
+                    src_ref=src, dst_ref=dst, send_sem=os_.at[b, a], recv_sem=or_.at[b, a],
+                    device_id=dev(f, to), device_id_type=MESH,
+                ).start()
+
+            if k:
+                far()
+                continue
+
+            pl.when(w != group)(far)
+
+            @pl.when(w == group)
+            def _(src=src, dst=dst):
+                pltpu.make_async_copy(src, dst, or_.at[b, a]).start()
 
     def spread(a, b):
         with jax.named_scope(f"hopwait{a}{b}"):
             ref = middle.at[pl.ds(0, 3), b, a]
             pltpu.make_async_copy(ref, ref, hr.at[b, a]).wait()
-
-        def source(to):
-            w, v = pick(to % NX, to // NX), pick(to // NX, to % NX)
-            return middle.at[w, b, a, v]
-
-        def go(t, carry):
-            to = line_peer(t)
-            pltpu.make_async_remote_copy(
-                src_ref=source(to), dst_ref=land_o.at[s, b, a],
-                send_sem=os_.at[b, a], recv_sem=or_.at[b, a],
-                device_id=dev(f, to), device_id_type=MESH,
-            ).start()
-            return carry
-
         with jax.named_scope(f"spread{a}{b}"):
-            for_peers(go)
-            pltpu.make_async_copy(source(s), land_o.at[s, b, a], or_.at[b, a]).start()
+            for ahead in AHEAD:
+                spread_from(ahead, a, b)
 
     def arrived(a, b):
         ref = land_o.at[:, b, a]
         with jax.named_scope(f"arrive{a}{b}"):
             pltpu.make_async_copy(ref, ref, or_.at[b, a]).wait()
 
-    def finish(a, b):
-        with jax.named_scope(f"fin{a}{b}"):
-            at = pl.ds(b * SUB, SUB)
-            rows_ = pl.ds(a * SUB, SUB)
-            slabs = butterfly([land_o[i, b, a] for i in range(NS)], 8)
+    def finish(tiles):
+        with jax.named_scope("fin" + "_".join(f"{a}{b}" for a, b in tiles)):
+            slabs = butterfly(
+                [jnp.concatenate([land_o[i, b, a] for a, b in tiles], axis=0) for i in range(NS)], 8
+            )
             mixed = jnp.concatenate(slabs, axis=0).astype(jnp.float32)
             scaled = unit_channels(mixed, mid_gain[...]).astype(jnp.bfloat16)
             res = jnp.dot(scaled, out_w[...], preferred_element_type=jnp.float32)
-            o_ref[rows_, at] = (res.reshape(SUB, SUB, W) * gate[rows_, at]).astype(jnp.bfloat16)
+            res = res.reshape(SUB, len(tiles), SUB, W)
+            for t, (a, b) in enumerate(tiles):
+                rows_, at = pl.ds(a * SUB, SUB), pl.ds(b * SUB, SUB)
+                o_ref[rows_, at] = (res[:, t] * gate[rows_, at]).astype(jnp.bfloat16)
 
     def make(a, b):
         product(a, b)
         hop(a, b)
 
-    def end(a, b):
-        arrived(a, b)
-        finish(a, b)
+    def end(*tiles):
+        for a, b in tiles:
+            arrived(a, b)
+        finish(tiles)
 
     def drain_tiles(tiles):
         for a, b in tiles:
@@ -355,8 +374,8 @@
     pass_on(4)
     gathered(3)
     make(0, 1)
+    make(1, 1)
     pass_on(5)
-    make(1, 1)
     spread(1, 0)
     pass_on(6)
     gathered(4)
@@ -371,19 +390,15 @@
     make(2, 2)
     spread(2, 0)
     spread(2, 1)
+    end((0, 0), (1, 0))
     spread(0, 2)
-    end(0, 0)
     spread(1, 2)
-    end(1, 0)
     spread(2, 2)
-    end(0, 1)
-    end(1, 1)
-    end(2, 0)
-    end(2, 1)
+    end((0, 1), (1, 1))
+    end((2, 0), (2, 1))
     drain()
-    end(0, 2)
-    end(1, 2)
-    end(2, 2)
+    end((0, 2), (1, 2))
+    end((2, 2))
 
     drain_tiles(((2, 1), (0, 2), (1, 2), (2, 2)))
 

time: 60.5 us -> 60.1 us (level)
  no operation moved by 1% of the time
where the time goes in v4:
time: 60.1 us; the launch traced here: 60 us
  Pallas kernels  59.1 us (98%)
  local copies, waits for them, and re-layouts  0.82 us (1%)
    pallas_call x1, Pallas kernels, per_device(): pl.pallas_call(kernel, out_shape=jax.ShapeDtypeStruct((BLK, BLK, W), bf),...  59.1 us

profile of v4, /device:TPU:1, one launch (start us, length us, event | category | flops | bytes accessed | tf_op | source)
XLA Modules:
  0.0 60.0 jit_solution(3767327703960370779)
XLA Ops:
  0.0 59.1 %shard_map.73 = bf16[48,48,128]{2,1,0:T(8,128)(2,1)S(1)} custom-call(bf16[48,48,128]{2,1,0:T(8,128)(2,1)} %x_hbm.1, f32[1,128]{1,0:T(1,128)} %bitcast.2, bf16[128,128]{1,0:T(8,128)(2,1)} %left_hbm.1, bf16[128,128]{1,0:T(8,128)(2,1)} %right_hbm.1, f32[1,128]{1,0:T(1,128)} %bitcast.3, bf16[128,128]{1,0:T(8,128)(2,1)} %out_hbm.1, bf16[128,128]{1,0:T(8,128)(2,1)} %gate_hbm.1), custom_call_target="tpu_custom_call" | custom-call | tf_op jit(solution)/shard_map/pallas_call | solution.py:409
  59.1 0.8 %copy.9 = bf16[48,48,128]{2,1,0:T(8,128)(2,1)} copy(bf16[48,48,128]{2,1,0:T(8,128)(2,1)S(1)} %shard_map.73) | data formatting | bytes 1179648

commit v5 on v4

--- a/solution.py
+++ b/solution.py
@@ -30,7 +30,7 @@
 PEERS = tuple((h, other) for other in (0, 1) for h in (4, 3, -3, 2, -2, 1, -1, 0) if (h, other) != (0, 0))
 
 
-AHEAD = (2, 1, 3)
+AHEAD = (3, 1, 2)
 
 
 def unit_channels(values, channel_gain):
@@ -87,6 +87,27 @@
         return pick(along_x, along_y) if which == 0 else pick(along_y, along_x)
 
 
+    barrier = pltpu.get_barrier_semaphore()
+
+    def greet(first, second):
+        pl.semaphore_signal(barrier, inc=1, device_id=dev(first, second), device_id_type=MESH)
+
+    def line_peer(t):
+        h, other = PEERS[t]
+        return ((s // 2 + h + 8) % 8) * 2 + (s + other) % 2
+
+    def for_peers(go):
+        for t in range(NS - 1):
+            go(t, 0)
+
+    for t in range(NS - 1):
+        greet(f, line_peer(t))
+    for step in (1, NX - 1):
+        for which in (0, 1):
+            greet(ring(which, step), s)
+    greet(ring(0, 2), s)
+
+
     loads = [
         pltpu.make_async_copy(src, dst, ls.at[n])
         for n, (src, dst) in enumerate((
@@ -99,22 +120,6 @@
     for load in loads:
         load.start()
 
-    barrier = pltpu.get_barrier_semaphore()
-
-    def greet(first, second):
-        pl.semaphore_signal(barrier, inc=1, device_id=dev(first, second), device_id_type=MESH)
-
-    def greet_line(t, carry):
-        greet(f, (s + t) % NS)
-        return carry
-
-    lax.fori_loop(1, NS, greet_line, 0)
-    for step in (1, NX - 1):
-        for which in (0, 1):
-            greet(ring(which, step), s)
-    greet(ring(0, 2), s)
-
-
     rows = lax.broadcasted_iota(jnp.int32, (W, W), 0)
     cols = lax.broadcasted_iota(jnp.int32, (W, W), 1)
     swap = (rows == (cols % 16) * 8 + cols // 16).astype(jnp.bfloat16)
@@ -122,14 +127,6 @@
     right_mix = jnp.dot(
         right_w[...], swap, preferred_element_type=jnp.float32
     ).astype(jnp.bfloat16)
-
-    def line_peer(t):
-        h, other = PEERS[t]
-        return ((s // 2 + h + 8) % 8) * 2 + (s + other) % 2
-
-    def for_peers(go):
-        for t in range(NS - 1):
-            go(t, 0)
 
     rows_s = pl.ds(pl.multiple_of(s * SUB, SUB), SUB)
 
@@ -395,10 +392,10 @@
     spread(1, 2)
     spread(2, 2)
     end((0, 1), (1, 1))
+    drain()
     end((2, 0), (2, 1))
-    drain()
-    end((0, 2), (1, 2))
-    end((2, 2))
+    end((0, 2))
+    end((1, 2), (2, 2))
 
     drain_tiles(((2, 1), (0, 2), (1, 2), (2, 2)))
 

time: 60.1 us -> 59.2 us (0.985)
  Pallas kernels: 59.1 us -> 58.2 us
    pallas_call x1, Pallas kernels: 59.1 us -> 58.2 us  [per_device(): pl.pallas_call(kernel, out_shape=jax.ShapeDtypeStruct((BLK, BLK, W), bf),...]
where the time goes in v5:
time: 59.2 us; the launch traced here: 59.1 us
  Pallas kernels  58.2 us (98%)
  local copies, waits for them, and re-layouts  0.82 us (1%)
    pallas_call x1, Pallas kernels, per_device(): pl.pallas_call(kernel, out_shape=jax.ShapeDtypeStruct((BLK, BLK, W), bf),...  58.2 us

profile of v5, /device:TPU:1, one launch (start us, length us, event | category | flops | bytes accessed | tf_op | source)
XLA Modules:
  0.0 59.1 jit_solution(586982856352931796)
XLA Ops:
  0.0 58.2 %shard_map.73 = bf16[48,48,128]{2,1,0:T(8,128)(2,1)S(1)} custom-call(bf16[48,48,128]{2,1,0:T(8,128)(2,1)} %x_hbm.1, f32[1,128]{1,0:T(1,128)} %bitcast.2, bf16[128,128]{1,0:T(8,128)(2,1)} %left_hbm.1, bf16[128,128]{1,0:T(8,128)(2,1)} %right_hbm.1, f32[1,128]{1,0:T(1,128)} %bitcast.3, bf16[128,128]{1,0:T(8,128)(2,1)} %out_hbm.1, bf16[128,128]{1,0:T(8,128)(2,1)} %gate_hbm.1), custom_call_target="tpu_custom_call" | custom-call | tf_op jit(solution)/shard_map/pallas_call | solution.py:406
  58.3 0.8 %copy.9 = bf16[48,48,128]{2,1,0:T(8,128)(2,1)} copy(bf16[48,48,128]{2,1,0:T(8,128)(2,1)S(1)} %shard_map.73) | data formatting | bytes 1179648

commit v6 on v5

--- a/solution.py
+++ b/solution.py
@@ -375,11 +375,11 @@
     pass_on(5)
     spread(1, 0)
     pass_on(6)
+    spread(0, 1)
     gathered(4)
     make(2, 0)
-    spread(0, 1)
+    spread(1, 1)
     make(2, 1)
-    spread(1, 1)
     gathered(5)
     gathered(6)
     make(0, 2)

time: 59.2 us -> 59 us (level)
  no operation moved by 1% of the time
where the time goes in v6:
time: 59 us; the launch traced here: 58.9 us
  Pallas kernels  58 us (98%)
  local copies, waits for them, and re-layouts  0.82 us (1%)
    pallas_call x1, Pallas kernels, per_device(): pl.pallas_call(kernel, out_shape=jax.ShapeDtypeStruct((BLK, BLK, W), bf),...  58 us

profile of v6, /device:TPU:1, one launch (start us, length us, event | category | flops | bytes accessed | tf_op | source)
XLA Modules:
  0.0 58.9 jit_solution(5750894942668334914)
XLA Ops:
  0.0 58.0 %shard_map.73 = bf16[48,48,128]{2,1,0:T(8,128)(2,1)S(1)} custom-call(bf16[48,48,128]{2,1,0:T(8,128)(2,1)} %x_hbm.1, f32[1,128]{1,0:T(1,128)} %bitcast.2, bf16[128,128]{1,0:T(8,128)(2,1)} %left_hbm.1, bf16[128,128]{1,0:T(8,128)(2,1)} %right_hbm.1, f32[1,128]{1,0:T(1,128)} %bitcast.3, bf16[128,128]{1,0:T(8,128)(2,1)} %out_hbm.1, bf16[128,128]{1,0:T(8,128)(2,1)} %gate_hbm.1), custom_call_target="tpu_custom_call" | custom-call | tf_op jit(solution)/shard_map/pallas_call | solution.py:406
  58.0 0.8 %copy.9 = bf16[48,48,128]{2,1,0:T(8,128)(2,1)} copy(bf16[48,48,128]{2,1,0:T(8,128)(2,1)S(1)} %shard_map.73) | data formatting | bytes 1179648
